TPU v7x, 256 devices: a whole 4x4x8 slice. The times are simulated.
256 devices in a mesh: grp: 8 (over z), row: 32 (over x, y, core).
Axes of the slice: x: 4, y: 4, z: 8, core: 2. Of those that a mesh axis runs over, the one named last changes fastest.
Arguments:
- expert_grams: float32 [4, 4096, 4096], P(None, 'row'), may hold values from -32 to 48, as said below
- expert_weights: bfloat16 [4, 4096, 1024], P(None, 'row', 'grp'), may hold values from -6 to 6
Outputs:
- merged: float32 [4096, 1024], P('row', 'grp')
- residual_ratio: float32 [], replicated
Inputs may be any that keep to these rules, and one draw needn't show every extreme that they name: Each expert_grams[k] is exactly symmetric and positive definite.
All inputs are finite; a program needn't handle non-finite values.
Results may differ from a plain program's by a relative error of at most 0.0003.
Values may be sent and summed in bfloat16 or wider, within the bound.
A program may use at most 64 MiB of HBM per device.

v0:
```python
import jax
import jax.numpy as jnp
from jax import lax
from jax.sharding import PartitionSpec as P

ITERS = 4


def sent_to_all(x, axis):
    copies = jnp.broadcast_to(x, (lax.axis_size(axis), *x.shape))
    return lax.all_to_all(copies, axis, split_axis=0, concat_axis=0, tiled=True)


def taken_together(x, axis):
    return sent_to_all(x, axis).sum(axis=0)


def in_one(arrays, axis):
    flat, at, outs = (jnp.concatenate([a.reshape(-1) for a in arrays]), 0, [])
    running = taken_together(flat, axis)
    for a in arrays:
        outs.append(running[at : at + a.size].reshape(a.shape))
        at += a.size
    return tuple(outs)


def split_up(x, dim, count):
    lengths = x.shape
    blocks = x.reshape(*lengths[:dim], count, lengths[dim] // count, *lengths[dim + 1 :])
    return jnp.moveaxis(blocks, dim, 0)


def summed_on_arrival(x, axis, dim):
    blocks = split_up(x, dim, lax.axis_size(axis))
    arrived = lax.all_to_all(blocks, axis, split_axis=0, concat_axis=0, tiled=True)
    return arrived.sum(axis=0)


def joined_along(blocks, dim):
    lengths = list(blocks.shape[1:])
    lengths[dim] *= blocks.shape[0]
    return jnp.moveaxis(blocks, 0, dim).reshape(lengths)


def collect(x, axis, dim):
    return joined_along(sent_to_all(x, axis), dim)


def both_sums(residual, mapped):
    return in_one((jnp.sum(residual * residual, axis=0), jnp.sum(residual * mapped, axis=0)), "row")


def local(expert_grams, expert_weights):
    rows_local = expert_grams.shape[1]
    full_width = expert_grams.shape[2]
    columns = expert_weights.shape[2]
    offset = lax.axis_index("row") * rows_local
    row_ids = offset + lax.broadcasted_iota(jnp.int32, (rows_local, full_width), 0)
    col_ids = lax.broadcasted_iota(jnp.int32, (rows_local, full_width), 1)
    system = jnp.sum(expert_grams, axis=0) + (row_ids == col_ids).astype(jnp.float32)
    empty = jnp.zeros((rows_local, columns), jnp.float32)
    local_weights = expert_weights.astype(jnp.float32)
    target = summed_on_arrival(
        jnp.einsum(
            "kjr,kjc->rc",
            expert_grams,
            local_weights,
            precision=lax.Precision.HIGHEST,
            preferred_element_type=jnp.float32,
        ),
        "row",
        0,
    )

    def add_panel(incoming):
        return jnp.dot(
            system, incoming, precision=lax.Precision.HIGHEST, preferred_element_type=jnp.float32
        )

    def apply_system(vectors):
        return add_panel(collect(vectors, "row", 0))

    merged = empty
    residual = target
    mapped = apply_system(residual)
    norm_now, product = both_sums(residual, mapped)
    initial = norm_now
    step_size = norm_now / product
    direction = residual
    mapped_dir = mapped
    for iteration in range(ITERS):
        merged = merged + step_size * direction
        residual = residual - step_size * mapped_dir
        if iteration + 1 < ITERS:
            mapped = apply_system(residual)
            norm_next, product = both_sums(residual, mapped)
            scaling = norm_next / norm_now
            step_size = norm_next / (product - scaling * norm_next / step_size)
            direction = residual + scaling * direction
            mapped_dir = mapped + scaling * mapped_dir
            norm_now = norm_next
    final_sums = taken_together(jnp.sum(residual * residual, axis=0), "row")
    totals = in_one((jnp.sum(final_sums), jnp.sum(initial)), "grp")
    residual_ratio = jnp.sqrt(totals[0] / totals[1])
    return (merged, residual_ratio)


def solution(mesh):
    placed = (P(None, "row", None), P(None, "row", "grp"))
    return jax.shard_map(
        local, mesh=mesh, in_specs=placed, out_specs=(P("row", "grp"), P()), check_vma=False
    )
```

profile of v0, /device:TPU:1, one launch (start us, length us, event | category | flops | bytes accessed | tf_op | source)
XLA Modules:
  0.0 265.0 jit_solution(16300284189341919301)
XLA Ops:
  0.6 0.9 copy-done
  1.5 9.1 %fusion.9 = f32[4096,128,1]{1,0,2:T(8,128)S(1)} fusion(f32[4,128,4096]{2,1,0:T(8,128)} %param.2, bf16[4,128,128]{2,1,0:T(8,128)(2,1)S(1)} %copy-done), kind=kOutput, calls=%fused_computation.42 | convolution fusion | flops 3221225472 | bytes 10616832 | tf_op jit(solution)/shard_map/kjr,kjc->rc/dot_general | solution.py:64
  10.6 36.5 %all_to_all.61 = f32[32,128,128]{2,1,0:T(8,128)S(1)} all-to-all(f32[32,128,128]{2,1,0:T(8,128)S(1)} %bitcast.20), channel_id=1, replica_groups=mesh['grp'=8,'row'=32] {'row'}, dimensions={0} | all-to-all | bytes 4194304 | tf_op jit(solution)/shard_map/all_to_all | solution.py:35
  47.2 0.1 reduce_sum.166
  47.3 1.5 broadcast_in_dim.20
  48.8 4.5 %all-to-all-start.1 = ((f32[32,128,128]{2,1,0:T(8,128)}), f32[32,128,128]{2,1,0:T(8,128)}, u32[]{:S(2)}, u32[]{:S(2)}) async-start(f32[32,128,128]{2,1,0:T(8,128)} %broadcast_in_dim.20), calls=%async_computation.1 | async-start | bytes 4194304 | tf_op jit(solution)/shard_map/all_to_all | solution.py:11
  53.4 4.2 %reduce_sum.168 = f32[128,4096]{1,0:T(8,128)S(1)} reduce(f32[4,128,4096]{2,1,0:T(8,128)} %param.2, f32[]{:T(128)} %constant.3.clone.1), dimensions={0}, to_apply=%region_2.0 | reduce | flops 1572864 | bytes 10485764 | tf_op jit(solution)/shard_map/reduce_sum | solution.py:60
  57.6 24.2 %all-to-all-done.1 = f32[32,128,128]{2,1,0:T(8,128)} async-done(((f32[32,128,128]{2,1,0:T(8,128)}), f32[32,128,128]{2,1,0:T(8,128)}, u32[]{:S(2)}, u32[]{:S(2)}) %all-to-all-start.1) | async-done | bytes 2097184 | tf_op jit(solution)/shard_map/all_to_all | solution.py:11
  81.7 4.0 %multiply_reduce_fusion.8 = (f32[128]{0:T(128)S(1)}, f32[128]{0:T(128)S(1)}, f32[128,128]{1,0:T(8,128)S(1)}) fusion(f32[128,128]{1,0:T(8,128)S(1)} %reduce_sum.166, f32[4096,128]{1,0:T(8,128)} %bitcast.2, f32[128,4096]{1,0:T(8,128)S(1)} %reduce_sum.168, s32[128]{0:T(128)S(1)} %iota_add_fusion), kind=kOutput, calls=%fused_computation.24 | convolution fusion | flops 806944512 | bytes 4326912 | tf_op jit(solution)/shard_map/dot_general | solution.py:76
  85.8 10.9 %all_to_all.62 = f32[32,1,256]{2,1,0:T(1,128)S(1)} all-to-all(f32[32,1,256]{2,1,0:T(1,128)S(1)} %broadcast_in_dim.21), channel_id=1, replica_groups=mesh['grp'=8,'row'=32] {'row'}, dimensions={0} | all-to-all | bytes 65536 | tf_op jit(solution)/shard_map/all_to_all | solution.py:11
  96.7 0.1 reduce_sum.170
  96.8 0.6 slice_reduce_fusion
  97.4 0.2 broadcast_in_dim.22
  97.6 31.6 %all_to_all.63 = f32[32,128,128]{2,1,0:T(8,128)S(1)} all-to-all(f32[32,128,128]{2,1,0:T(8,128)S(1)} %broadcast_in_dim.22), channel_id=1, replica_groups=mesh['grp'=8,'row'=32] {'row'}, dimensions={0} | all-to-all | bytes 4194304 | tf_op jit(solution)/shard_map/all_to_all | solution.py:11
  129.2 2.5 multiply_reduce_fusion.6
  131.8 11.2 %all_to_all.64 = f32[32,1,256]{2,1,0:T(1,128)S(1)} all-to-all(f32[32,1,256]{2,1,0:T(1,128)S(1)} %broadcast_in_dim.23), channel_id=1, replica_groups=mesh['grp'=8,'row'=32] {'row'}, dimensions={0} | all-to-all | bytes 65536 | tf_op jit(solution)/shard_map/all_to_all | solution.py:11
  142.9 0.1 reduce_sum.173
  143.0 0.2 broadcast_in_dim.48
  143.3 31.6 %all_to_all.65 = f32[32,128,128]{2,1,0:T(8,128)S(1)} all-to-all(f32[32,128,128]{2,1,0:T(8,128)S(1)} %broadcast_in_dim.48), channel_id=1, replica_groups=mesh['grp'=8,'row'=32] {'row'}, dimensions={0} | all-to-all | bytes 4194304 | tf_op jit(solution)/shard_map/all_to_all | solution.py:11
  174.9 2.5 multiply_reduce_fusion.4
  177.4 11.0 %all_to_all.66 = f32[32,1,256]{2,1,0:T(1,128)S(1)} all-to-all(f32[32,1,256]{2,1,0:T(1,128)S(1)} %broadcast_in_dim.49), channel_id=1, replica_groups=mesh['grp'=8,'row'=32] {'row'}, dimensions={0} | all-to-all | bytes 65536 | tf_op jit(solution)/shard_map/all_to_all | solution.py:11
  188.4 0.1 reduce_sum.176
  188.5 0.2 broadcast_in_dim.50
  188.8 31.6 %all_to_all.67 = f32[32,128,128]{2,1,0:T(8,128)S(1)} all-to-all(f32[32,128,128]{2,1,0:T(8,128)S(1)} %broadcast_in_dim.50), channel_id=1, replica_groups=mesh['grp'=8,'row'=32] {'row'}, dimensions={0} | all-to-all | bytes 4194304 | tf_op jit(solution)/shard_map/all_to_all | solution.py:11
  220.4 2.5 multiply_reduce_fusion.2
  222.9 11.0 %all_to_all.68 = f32[32,1,256]{2,1,0:T(1,128)S(1)} all-to-all(f32[32,1,256]{2,1,0:T(1,128)S(1)} %broadcast_in_dim.51), channel_id=1, replica_groups=mesh['grp'=8,'row'=32] {'row'}, dimensions={0} | all-to-all | bytes 65536 | tf_op jit(solution)/shard_map/all_to_all | solution.py:11
  234.0 0.7 multiply_reduce_fusion
  234.7 10.4 %all_to_all.69 = f32[32,1,128]{2,1,0:T(1,128)S(1)} all-to-all(f32[32,1,128]{2,1,0:T(1,128)S(1)} %broadcast_in_dim.52), channel_id=1, replica_groups=mesh['grp'=8,'row'=32] {'row'}, dimensions={0} | all-to-all | bytes 32768 | tf_op jit(solution)/shard_map/all_to_all | solution.py:11
  245.2 0.7 reduce_sum.181
  245.8 1.4 pad_maximum_fusion.4
  247.3 14.5 %all_to_all.70 = f32[8,1,2]{2,1,0:T(1,128)S(1)} all-to-all(f32[8,1,2]{2,1,0:T(1,128)S(1)} %broadcast_in_dim.53), channel_id=1, replica_groups=mesh['grp'=8,'row'=32] {'grp'}, dimensions={0} | all-to-all | bytes 128 | tf_op jit(solution)/shard_map/all_to_all | solution.py:11
  261.8 0.6 fusion.8
  (20 shorter events, 0.3 us)
Async XLA Ops:
  0.6 0.9 copy-start
  48.8 32.9 %all-to-all-start.1 = ((f32[32,128,128]{2,1,0:T(8,128)}), f32[32,128,128]{2,1,0:T(8,128)}, u32[]{:S(2)}, u32[]{:S(2)}) async-start(f32[32,128,128]{2,1,0:T(8,128)} %broadcast_in_dim.20), calls=%async_computation.1 | async-start | bytes 4194304 | tf_op jit(solution)/shard_map/all_to_all | solution.py:11
where the time goes:
time: 266 us; the launch traced here: 265 us
  blocking collectives  200 us (75%)
  waiting for transfers between devices  24.2 us (9%)
  matrix products  20.6 us (8%)
  other arithmetic  8.06 us (3%)
  starting transfers between devices  4.54 us (2%)
  local copies, waits for them, and re-layouts  3.81 us (1%)
  between operations  3.32 us (1%)
    all_to_all x9, blocking collectives, sent_to_all(): return lax.all_to_all(copies, axis, split_axis=0, concat_axis=0, tiled=True)  164 us
    all_to_all x1, blocking collectives, summed_on_arrival(): lax.all_to_all(blocks, axis, split_axis=0, concat_axis=0, tiled=True)  36.5 us
    all_to_all x1, waiting for transfers between devices, sent_to_all(): return lax.all_to_all(copies, axis, split_axis=0, concat_axis=0, tiled=True)  24.2 us
    dot_general x4, matrix products, add_panel(): jnp.dot(system, incoming, precision=lax.Precision.HIGHEST, preferred_elem...  11.5 us
    dot_general x1, matrix products, local(): jnp.einsum('kjr,kjc->rc', expert_grams, local_weights, precision=lax.Prec...  9.09 us
  transfers between devices with their start and end apart: 1, of which 1 were waited for; matrix products, arithmetic and copies ran while one was open for 2% of the time, Pallas kernels for 0%

commit v1 on v0

v1 whole, which is shorter than its diff:
```python
import jax
import jax.numpy as jnp
from jax import lax
from jax.experimental import pallas as pl
from jax.experimental.pallas import tpu as pltpu
from jax.sharding import PartitionSpec as P

MESH = pl.DeviceIdType.MESH
F32, BF16 = jnp.float32, jnp.bfloat16
EXPERTS, ROWS, COLS = 4, 128, 128
CHIPS, SIDE, WIDE, MINE, HALF = 16, 4, 256, 64, 32


def split(x):
    high = x.astype(BF16)
    return high, (x - high.astype(F32)).astype(BF16)


def column_sum(x):
    return jnp.sum(x, axis=1, keepdims=True)


def kernel(
    grams, weights, merged, ratio,
    panel, matrix, weights_t, partial, partner_part, first, second, outgoing,
    gather_b, gather_0, gather_1, gather_2, residual, mapped_dir,
    sums, totals, answer,
    panel_sem, partner_sem, matrix_sem, first_sem, second_sem, gather_sem, sums_sem, totals_sem, answer_sem, send_sem,
):
    grp, row = lax.axis_index("grp"), lax.axis_index("row")
    core, chip = lax.rem(row, 2), lax.div(row, 2)
    x, y = lax.div(chip, SIDE), lax.rem(chip, SIDE)
    other = 1 - core

    def at(cx, cy):
        return lax.rem(cx, SIDE) * SIDE + lax.rem(cy, SIDE)

    def device(target):
        return (grp, target * 2 + core)

    partner = (grp, chip * 2 + other)

    def push(src, dst, sent, arrived, to):
        pltpu.make_async_remote_copy(src, dst, sent, arrived, device_id=to, device_id_type=MESH).start()

    def await_bytes(ref, sem):
        pltpu.make_async_copy(ref, ref, sem).wait()

    def order(n):
        return lax.rem(chip + 1 + n, CHIPS)

    def panel_copy(n):
        columns = pl.ds(pl.multiple_of(order(n) * WIDE, WIDE), WIDE)
        return pltpu.make_async_copy(grams.at[:, :, columns], panel.at[n], panel_sem.at[n])

    def fetch(n, _):
        panel_copy(n).start()
        return 0

    lax.fori_loop(0, CHIPS, fetch, 0)

    barrier = pltpu.get_barrier_semaphore()

    def greet_chip(n, _):
        pl.semaphore_signal(barrier, 1, device_id=device(lax.rem(chip + n, CHIPS)), device_id_type=MESH)
        return 0

    lax.fori_loop(1, CHIPS, greet_chip, 0)
    groups = lax.axis_size("grp")

    def greet_group(n, _):
        there = lax.rem(grp * 2 + core + n, 2 * groups)
        pl.semaphore_signal(
            barrier, 1, device_id=(lax.div(there, 2), chip * 2 + lax.rem(there, 2)), device_id_type=MESH
        )
        return 0

    lax.fori_loop(1, 2 * groups, greet_group, 0)

    stacked = weights[...].reshape(EXPERTS * ROWS, COLS).astype(F32)
    weights_t[...] = jnp.transpose(stacked).astype(BF16)
    pl.semaphore_wait(barrier, CHIPS - 1 + 2 * groups - 1)

    def compute_panel(n):
        target = order(n)
        panel_copy(n).wait()
        block = panel[n].reshape(EXPERTS * ROWS, WIDE)
        high, low = split(block)
        product = jnp.dot(weights_t[...], high, preferred_element_type=F32) + jnp.dot(
            weights_t[...], low, preferred_element_type=F32
        )
        partial[target] = product.reshape(2, MINE, WIDE)
        push(partial.at[target, other], partner_part.at[target], send_sem.at[0], partner_sem.at[target], partner)
        system = (panel[n, 0] + panel[n, 1]) + (panel[n, 2] + panel[n, 3])
        rows = lax.broadcasted_iota(jnp.int32, (ROWS, WIDE), 0) + (chip * WIDE + core * ROWS)
        columns = lax.broadcasted_iota(jnp.int32, (ROWS, WIDE), 1) + target * WIDE
        system = system + (rows == columns).astype(F32)
        system_high, system_low = split(system)
        matrix[target, core, 0] = system_high
        matrix[target, core, 1] = system_low
        push(matrix.at[target, core], matrix.at[target, core], send_sem.at[1], matrix_sem.at[target], partner)

    def forward_panel(n):
        target = order(n)
        tx, ty = lax.div(target, SIDE), lax.rem(target, SIDE)
        await_bytes(partner_part.at[target], partner_sem.at[target])
        outgoing[target] = partial[target, core] + partner_part[target]

        @pl.when(tx != x)
        def _():
            push(
                outgoing.at[target, pl.ds(0, HALF)], first.at[0, x, ty],
                send_sem.at[2], first_sem.at[0, x, ty], device(at(tx, y)),
            )

        @pl.when(ty != y)
        def _():
            push(
                outgoing.at[target, pl.ds(HALF, HALF)], first.at[1, y, tx],
                send_sem.at[2], first_sem.at[1, y, tx], device(at(x, ty)),
            )

    lag = 2

    def panel_step(n, _):
        @pl.when(n < CHIPS)
        def _():
            compute_panel(n)

        @pl.when(n >= lag)
        def _():
            forward_panel(n - lag)

        return 0

    lax.fori_loop(0, CHIPS + lag, panel_step, 0)

    def first_sum(half, k):
        line, along = (x, y) if half == 0 else (y, x)
        place = lax.rem(along + k, SIDE)
        target = at(x, place) if half == 0 else at(place, y)
        total = outgoing[target, pl.ds(half * HALF, HALF)]
        for j in (1, 3, 2):
            source = lax.rem(line + j, SIDE)
            await_bytes(first.at[half, source, place], first_sem.at[half, source, place])
            total = total + first[half, source, place]
        return total, target

    for k in (1, 3, 2):
        for half in (0, 1):
            along = y if half == 0 else x
            total, target = first_sum(half, k)
            second[half, 0, k] = total
            push(
                second.at[half, 0, k], second.at[half, 1, along],
                send_sem.at[3], second_sem.at[half, along], device(target),
            )
    pieces = []
    for half in (0, 1):
        along = y if half == 0 else x
        total, _ = first_sum(half, 0)
        for j in (1, 3, 2):
            source = lax.rem(along + j, SIDE)
            await_bytes(second.at[half, 1, source], second_sem.at[half, source])
            total = total + second[half, 1, source]
        pieces.append(total)
    own_r = jnp.concatenate(pieces, axis=0)

    def gather(index, buffer, value):
        if index < 3:
            high, low = split(value)
            for half in (0, 1):
                buffer[chip, half, 0] = high[half * HALF : (half + 1) * HALF]
                buffer[chip, half, 1] = low[half * HALF : (half + 1) * HALF]
        else:
            high = value.astype(BF16)
            for half in (0, 1):
                buffer[chip, half] = high[half * HALF : (half + 1) * HALF]

        def send(origin, half, target):
            block = buffer.at[origin, half]
            push(block, block, send_sem.at[4 + index], gather_sem.at[index, origin, half], device(target))

        def arrive(origin, half):
            await_bytes(buffer.at[origin, half], gather_sem.at[index, origin, half])

        steps = (1, 3, 2)
        for d in steps:
            send(chip, 0, at(x + d, y))
            send(chip, 1, at(x, y + d))
        for d in steps:
            send(chip, 0, at(x, y + d))
            send(chip, 1, at(x + d, y))
        for d in (3, 1, 2):
            origin = at(x + d, y)
            arrive(origin, 0)
            for e in steps:
                send(origin, 0, at(x, y + e))
            origin = at(x, y + d)
            arrive(origin, 1)
            for e in steps:
                send(origin, 1, at(x + e, y))

        def finish():
            for d in (0, 1, 3, 2):
                for e in (1, 3, 2):
                    arrive(at(x + d, y + e), 0)
                    arrive(at(x + e, y + d), 1)

        return finish

    def multiply(buffer, planes):
        height = planes * MINE
        total = None
        for q in range(SIDE):
            left = jnp.concatenate([buffer[SIDE * q + i].reshape(height, WIDE) for i in range(SIDE)], axis=1)
            right = jnp.concatenate([matrix[SIDE * q + i].reshape(2 * WIDE, WIDE) for i in range(SIDE)], axis=1)
            piece = lax.dot_general(left, right, (((1,), (1,)), ((), ())), preferred_element_type=F32)
            total = piece if total is None else total + piece
        if planes == 2:
            total = total.reshape(2, 2, HALF, 2 * WIDE)
            total = (total[:, 0] + total[:, 1]).reshape(MINE, 2 * WIDE)
        return jnp.concatenate(
            [total[:, i * WIDE : i * WIDE + ROWS] + total[:, i * WIDE + ROWS : (i + 1) * WIDE] for i in (0, 1)],
            axis=1,
        )

    def whole(buffer, planes, origin):
        if planes == 2:
            block = buffer[origin].astype(F32)
            return (block[:, 0] + block[:, 1]).reshape(MINE, WIDE)
        return buffer[origin].astype(F32).reshape(MINE, WIDE)

    zero = jnp.zeros((MINE, WIDE), F32)

    gather(0, gather_b, own_r)()
    for origin in range(CHIPS):
        await_bytes(matrix.at[origin, other], matrix_sem.at[origin])

    def load_target(origin, total):
        block = whole(gather_b, 2, origin)
        residual[origin] = block
        return total + block * block

    norm = column_sum(lax.fori_loop(0, CHIPS, load_target, zero))
    initial = norm
    own_w = multiply(gather_b, 2)

    alpha = beta = None
    own_p = own_s = own_t = own_x = None
    for step, (buffer, planes) in enumerate(((gather_0, 2), (gather_1, 2), (gather_2, 1))):
        gather(step + 1, buffer, own_w)()

        def inner(origin, total, buffer=buffer, planes=planes):
            return total + residual[origin] * whole(buffer, planes, origin)

        product = column_sum(lax.fori_loop(0, CHIPS, inner, zero))
        own_u = multiply(buffer, planes)
        if step == 0:
            alpha = norm / product
            own_p, own_s, own_t = own_r, own_w, own_u
            own_x = alpha * own_p
        else:
            alpha = norm / (product - beta * norm / alpha)
            own_p = own_r + beta * own_p
            own_s = own_w + beta * own_s
            own_t = own_u + beta * own_t
            own_x = own_x + alpha * own_p
        own_r = own_r - alpha * own_s
        own_w = own_w - alpha * own_t

        def advance(origin, total, buffer=buffer, planes=planes, step=step, alpha=alpha, beta=beta):
            direction = whole(buffer, planes, origin)
            if step > 0:
                direction = direction + beta * mapped_dir[origin]
            mapped_dir[origin] = direction
            block = residual[origin] - alpha * direction
            residual[origin] = block
            return total + block * block

        following = column_sum(lax.fori_loop(0, CHIPS, advance, zero))
        beta = following / norm
        norm = following

    own_s = own_w + beta * own_s
    own_p = own_r + beta * own_p
    near = own_r - alpha * own_s
    lane = lax.broadcasted_iota(jnp.int32, (MINE, ROWS), 1)
    packed = jnp.zeros((MINE, ROWS), F32)
    for i, terms in enumerate((own_r * own_w, near * near, near * own_s, own_s * own_s)):
        packed = jnp.where(lane == i, column_sum(terms), packed)
    packed = jnp.transpose(jnp.concatenate([packed, jnp.zeros_like(packed)], axis=0))
    sums[chip] = packed[:8]

    def tell_chip(n, _):
        push(sums.at[chip], sums.at[chip], send_sem.at[8], sums_sem.at[chip], device(lax.rem(chip + n, CHIPS)))
        return 0

    lax.fori_loop(1, CHIPS, tell_chip, 0)

    def hear_chip(n, _):
        source = lax.rem(chip + n, CHIPS)
        await_bytes(sums.at[source], sums_sem.at[source])
        return 0

    lax.fori_loop(1, CHIPS, hear_chip, 0)
    gathered = jnp.sum(sums[...], axis=0)
    gathered = jnp.transpose(jnp.concatenate([gathered, jnp.zeros((ROWS - 8, ROWS), F32)], axis=0))[:MINE]
    product, near_near, near_s, s_s = (gathered[:, i : i + 1] for i in range(4))
    last = norm / (product - beta * norm / alpha)
    own_x = own_x + last * own_p
    excess = last - alpha
    final = jnp.maximum(near_near - 2.0 * excess * near_s + excess * excess * s_s, 0.0)

    place = grp * 2 + core
    lane = lax.broadcasted_iota(jnp.int32, (MINE, ROWS), 1)
    both = jnp.where(lane == 0, final, jnp.where(lane == 1, initial, 0.0))
    totals[place] = jnp.sum(both, axis=0, keepdims=True)
    answer[core, 0] = own_x[:, :ROWS]
    answer[core, 1] = own_x[:, ROWS:]
    push(answer.at[core, other], answer.at[core, other], send_sem.at[9], answer_sem, partner)

    def tell_group(n, _):
        there = lax.rem(place + n, 2 * groups)
        push(
            totals.at[place], totals.at[place], send_sem.at[10], totals_sem.at[place],
            (lax.div(there, 2), chip * 2 + lax.rem(there, 2)),
        )
        return 0

    lax.fori_loop(1, 2 * groups, tell_group, 0)
    await_bytes(answer.at[other, core], answer_sem)
    columns = jnp.concatenate([answer[0, core], answer[1, core]], axis=0)
    merged[...] = jnp.transpose(columns)

    def hear_group(n, _):
        source = lax.rem(place + n, 2 * groups)
        await_bytes(totals.at[source], totals_sem.at[source])
        return 0

    lax.fori_loop(1, 2 * groups, hear_group, 0)
    over_all = jnp.sum(totals[...], axis=0)
    ratio[...] = jnp.sqrt(over_all[:, 0:1] / over_all[:, 1:2]) + jnp.zeros((1, ROWS), F32)

    await_bytes(partner_part, send_sem.at[0])
    await_bytes(matrix.at[:, 0], send_sem.at[1])
    await_bytes(first.at[:, pl.ds(0, 3)], send_sem.at[2])
    await_bytes(second.at[:, 0, pl.ds(0, 3)], send_sem.at[3])
    for i, buffer in enumerate((gather_b, gather_0, gather_1, gather_2)):
        await_bytes(buffer.at[pl.ds(0, CHIPS - 1)], send_sem.at[4 + i])
    await_bytes(sums.at[pl.ds(0, CHIPS - 1)], send_sem.at[8])
    await_bytes(answer.at[0, 0], send_sem.at[9])
    await_bytes(totals.at[pl.ds(0, 2 * groups - 1)], send_sem.at[10])


def local(expert_grams, expert_weights):
    groups = lax.axis_size("grp")
    vmem = pl.BlockSpec(memory_space=pltpu.VMEM)
    dma = pltpu.SemaphoreType.DMA
    merged, ratio = pl.pallas_call(
        kernel,
        out_shape=(jax.ShapeDtypeStruct((ROWS, COLS), F32), jax.ShapeDtypeStruct((1, ROWS), F32)),
        in_specs=[pl.BlockSpec(memory_space=pl.ANY), vmem],
        out_specs=(vmem, vmem),
        scratch_shapes=[
            pltpu.VMEM((CHIPS, EXPERTS, ROWS, WIDE), F32),
            pltpu.VMEM((CHIPS, 2, 2, ROWS, WIDE), BF16),
            pltpu.VMEM((COLS, EXPERTS * ROWS), BF16),
            pltpu.VMEM((CHIPS, 2, MINE, WIDE), F32),
            pltpu.VMEM((CHIPS, MINE, WIDE), F32),
            pltpu.VMEM((2, SIDE, SIDE, HALF, WIDE), F32),
            pltpu.VMEM((2, 2, SIDE, HALF, WIDE), F32),
            pltpu.VMEM((CHIPS, MINE, WIDE), F32),
            pltpu.VMEM((CHIPS, 2, 2, HALF, WIDE), BF16),
            pltpu.VMEM((CHIPS, 2, 2, HALF, WIDE), BF16),
            pltpu.VMEM((CHIPS, 2, 2, HALF, WIDE), BF16),
            pltpu.VMEM((CHIPS, 2, HALF, WIDE), BF16),
            pltpu.VMEM((CHIPS, MINE, WIDE), F32),
            pltpu.VMEM((CHIPS, MINE, WIDE), F32),
            pltpu.VMEM((CHIPS, 8, ROWS), F32),
            pltpu.VMEM((2 * groups, 1, ROWS), F32),
            pltpu.VMEM((2, 2, MINE, ROWS), F32),
            dma((CHIPS,)),
            dma((CHIPS,)),
            dma((CHIPS,)),
            dma((2, SIDE, SIDE)),
            dma((2, SIDE)),
            dma((4, CHIPS, 2)),
            dma((CHIPS,)),
            dma((2 * groups,)),
            dma,
            dma((11,)),
        ],
        compiler_params=pltpu.CompilerParams(
            collective_id=0, has_side_effects=True, vmem_limit_bytes=56 * 1024 * 1024
        ),
        name="merge",
    )(expert_grams, expert_weights)
    return merged, ratio[0, 0]


def solution(mesh):
    placed = (P(None, "row", None), P(None, "row", "grp"))
    return jax.shard_map(
        local, mesh=mesh, in_specs=placed, out_specs=(P("row", "grp"), P()), check_vma=False
    )
```

time: 266 us -> 89.6 us (0.34)
  blocking collectives: 200 us -> 0 us
  Pallas kernels: 0 us -> 85.6 us
  waiting for transfers between devices: 24.2 us -> 0 us
  matrix products: 20.6 us -> 0 us
  other arithmetic: 8.06 us -> 0 us
  starting transfers between devices: 4.54 us -> 0 us
    all_to_all x10 -> x0, blocking collectives: 200 us -> none  [the longest x9 164 us: sent_to_all(): return lax.all_to_all(copies, axis, split_axis=0, concat_axis=0, tiled=True)]
    pallas_call x0 -> x1, Pallas kernels: none -> 85.6 us  [local(): pl.pallas_call(kernel, out_shape=(jax.ShapeDtypeStruct((ROWS, COLS), F32)...]
    all_to_all x1 -> x0, waiting for transfers between devices: 24.2 us -> none  [sent_to_all(): return lax.all_to_all(copies, axis, split_axis=0, concat_axis=0, tiled=True)]
    dot_general x5 -> x0, matrix products: 20.6 us -> none  [the longest x4 11.5 us: add_panel(): jnp.dot(system, incoming, precision=lax.Precision.HIGHEST, preferred_elem...]
    reduce_sum x10 -> x0, other arithmetic: 6.51 us -> none  [the longest x1 4.18 us: local(): jnp.sum(expert_grams, axis=0) + (row_ids == col_ids).astype(jnp.float32)]
    all_to_all x1 -> x0, starting transfers between devices: 4.54 us -> none  [sent_to_all(): return lax.all_to_all(copies, axis, split_axis=0, concat_axis=0, tiled=True)]
  transfers between devices with their start and end apart: 1 -> 0, of which waited for: 1 -> 0; matrix products, arithmetic and copies ran while one was open for 2% -> 0% of each run, Pallas kernels for 0% -> 0%
where the time goes in v1:
time: 89.6 us; the launch traced here: 89.4 us
  Pallas kernels  85.6 us (96%)
  between operations  2.39 us (3%)
  local copies, waits for them, and re-layouts  1.47 us (2%)
    pallas_call x1, Pallas kernels, local(): pl.pallas_call(kernel, out_shape=(jax.ShapeDtypeStruct((ROWS, COLS), F32)...  85.6 us

profile of v1, /device:TPU:1, one launch (start us, length us, event | category | flops | bytes accessed | tf_op | source)
XLA Modules:
  0.0 89.4 jit_solution(14715515707289467249)
XLA Ops:
  0.6 85.6 %merge.1 = (f32[128,128]{1,0:T(8,128)}, f32[1,128]{1,0:T(1,128)}) custom-call(f32[4,128,4096]{2,1,0:T(8,128)} %grams.1, bf16[4,128,128]{2,1,0:T(8,128)(2,1)} %weights.1), custom_call_target="tpu_custom_call" | custom-call | tf_op jit(solution)/shard_map/merge/pallas_call | solution.py:360
  86.2 1.5 %copy.6 = f32[128,128]{1,0:T(8,128)} copy(f32[128,128]{1,0:T(8,128)} %get-tuple-element.8) | data formatting | bytes 131072

commit v2 on v1

v2 whole, which is shorter than its diff:
```python
import jax
import jax.numpy as jnp
from jax import lax
from jax.experimental import pallas as pl
from jax.experimental.pallas import tpu as pltpu
from jax.sharding import PartitionSpec as P

MESH = pl.DeviceIdType.MESH
F32, BF16 = jnp.float32, jnp.bfloat16
EXPERTS, ROWS, COLS = 4, 128, 128
CHIPS, SIDE, WIDE, MINE, HALF = 16, 4, 256, 64, 32


def split(x):
    high = x.astype(BF16)
    return high, (x - high.astype(F32)).astype(BF16)


def column_sum(x):
    return jnp.sum(x, axis=1, keepdims=True)


def kernel(
    grams, weights, merged, ratio,
    panel, matrix, weights_in, weights_t, partial, partner_part, first, second, outgoing,
    gather_b, gather_0, gather_1, gather_2, residual, mapped_dir, dots, product,
    sums, totals, answer, merged_out, ratio_out,
    panel_sem, partner_sem, matrix_sem, first_sem, second_sem, gather_sem, sums_sem, totals_sem, answer_sem,
    send_sem, local_sem,
):
    grp, row = lax.axis_index("grp"), lax.axis_index("row")
    core, chip = lax.rem(row, 2), lax.div(row, 2)
    x, y = lax.div(chip, SIDE), lax.rem(chip, SIDE)
    other = 1 - core

    def at(cx, cy):
        return lax.rem(cx, SIDE) * SIDE + lax.rem(cy, SIDE)

    def device(target):
        return (grp, target * 2 + core)

    partner = (grp, chip * 2 + other)

    def push(src, dst, sent, arrived, to):
        pltpu.make_async_remote_copy(src, dst, sent, arrived, device_id=to, device_id_type=MESH).start()

    def await_bytes(ref, sem):
        pltpu.make_async_copy(ref, ref, sem).wait()

    weights_copy = pltpu.make_async_copy(weights, weights_in, local_sem.at[0])
    weights_copy.start()

    def panel_copy(n):
        columns = pl.ds(pl.multiple_of(n * WIDE, WIDE), WIDE)
        return pltpu.make_async_copy(grams.at[:, :, columns], panel.at[n], panel_sem.at[n])

    def fetch(n, _):
        panel_copy(n).start()
        return 0

    lax.fori_loop(0, CHIPS, fetch, 0)

    barrier = pltpu.get_barrier_semaphore()

    def greet_chip(n, _):
        pl.semaphore_signal(barrier, 1, device_id=device(lax.rem(chip + n, CHIPS)), device_id_type=MESH)
        return 0

    lax.fori_loop(1, CHIPS, greet_chip, 0)
    groups = lax.axis_size("grp")

    def greet_group(n, _):
        there = lax.rem(grp * 2 + core + n, 2 * groups)
        pl.semaphore_signal(
            barrier, 1, device_id=(lax.div(there, 2), chip * 2 + lax.rem(there, 2)), device_id_type=MESH
        )
        return 0

    lax.fori_loop(1, 2 * groups, greet_group, 0)

    weights_copy.wait()
    turned = jnp.transpose(weights_in[...].reshape(EXPERTS * ROWS, COLS).astype(F32)).astype(BF16)
    weights_t[:, : EXPERTS * ROWS] = turned
    weights_t[:, EXPERTS * ROWS :] = turned

    def compute_panel(target):
        panel_copy(target).wait()
        high, low = split(panel[target].reshape(EXPERTS * ROWS, WIDE))
        product = jnp.dot(weights_t[...], jnp.concatenate([high, low], axis=0), preferred_element_type=F32)
        partial[target] = product.reshape(2, MINE, WIDE)
        system = (panel[target, 0] + panel[target, 1]) + (panel[target, 2] + panel[target, 3])
        rows = lax.broadcasted_iota(jnp.int32, (ROWS, WIDE), 0) + (chip * WIDE + core * ROWS)
        columns = lax.broadcasted_iota(jnp.int32, (ROWS, WIDE), 1) + target * WIDE
        system_high, system_low = split(system + (rows == columns).astype(F32))
        matrix[target, core, 0] = system_high
        matrix[target, core, 1] = system_low

    def panel_step(n, _):
        for i in range(4):
            compute_panel(4 * n + i)
        return 0

    lax.fori_loop(0, CHIPS // 4, panel_step, 0)

    pl.semaphore_wait(barrier, CHIPS - 1 + 2 * groups - 1)

    targets = [(2, 2), (1, 2), (3, 2), (2, 1), (2, 3), (1, 1), (3, 1), (1, 3), (3, 3)]
    targets += [(0, 2), (2, 0), (0, 1), (1, 0), (0, 3), (3, 0), (0, 0)]
    for dx, dy in targets:
        target = at(x + dx, y + dy)
        push(partial.at[target, other], partner_part.at[target], send_sem.at[0], partner_sem.at[target], partner)
    for dx, dy in targets:
        target = at(x + dx, y + dy)
        await_bytes(partner_part.at[target], partner_sem.at[target])
        outgoing[target] = partial[target, core] + partner_part[target]
        if dx != 0:
            push(
                outgoing.at[target, pl.ds(0, HALF)], first.at[0, x, lax.rem(y + dy, SIDE)],
                send_sem.at[2], first_sem.at[0, x, lax.rem(y + dy, SIDE)], device(at(x + dx, y)),
            )
        if dy != 0:
            push(
                outgoing.at[target, pl.ds(HALF, HALF)], first.at[1, y, lax.rem(x + dx, SIDE)],
                send_sem.at[2], first_sem.at[1, y, lax.rem(x + dx, SIDE)], device(at(x, y + dy)),
            )

    def first_sum(half, k):
        line, along = (x, y) if half == 0 else (y, x)
        place = lax.rem(along + k, SIDE)
        target = at(x, place) if half == 0 else at(place, y)
        total = outgoing[target, pl.ds(half * HALF, HALF)]
        for j in (1, 3, 2):
            source = lax.rem(line + j, SIDE)
            await_bytes(first.at[half, source, place], first_sem.at[half, source, place])
            total = total + first[half, source, place]
        return total, target

    for k in (2, 1, 3):
        for half in (0, 1):
            along = y if half == 0 else x
            total, target = first_sum(half, k)
            second[half, 0, k] = total
            push(
                second.at[half, 0, k], second.at[half, 1, along],
                send_sem.at[3], second_sem.at[half, along], device(target),
            )
    def send_matrix(target, _):
        push(matrix.at[target, core], matrix.at[target, core], send_sem.at[1], matrix_sem, partner)
        return 0

    lax.fori_loop(0, CHIPS, send_matrix, 0)

    pieces = []
    for half in (0, 1):
        along = y if half == 0 else x
        total, _ = first_sum(half, 0)
        for j in (1, 3, 2):
            source = lax.rem(along + j, SIDE)
            await_bytes(second.at[half, 1, source], second_sem.at[half, source])
            total = total + second[half, 1, source]
        pieces.append(total)
    own_r = jnp.concatenate(pieces, axis=0)

    near_blocks = [(0, 0), (1, 0), (3, 0), (0, 1), (0, 3), (2, 0), (0, 2)]
    middle_blocks = [(1, 1), (1, 3), (3, 1), (3, 3)]
    far_blocks = [(2, 1), (2, 3), (1, 2), (3, 2), (2, 2)]

    def place_of(dx, dy, half):
        if dx != 0 and dy != 0:
            return 0 if 2 in (dx, dy) else 8
        if half == 0:
            return dx if dy == 0 else 7
        return 3 + dy if dx == 0 else 7

    class Gather:
        def __init__(self, index, buffer):
            self.index, self.buffer = index, buffer

        def send(self, dx, dy, half, ex, ey):
            block = self.buffer.at[at(x + dx, y + dy), half]
            place = place_of((dx - ex) % SIDE, (dy - ey) % SIDE, half)
            push(block, block, send_sem.at[4 + self.index], gather_sem.at[self.index, place], device(at(x + ex, y + ey)))

        def arrive(self, place, ref):
            await_bytes(ref, gather_sem.at[self.index, place])

        def start(self, value):
            buffer = self.buffer
            high, low = split(value)
            for half in (0, 1):
                here = slice(half * HALF, (half + 1) * HALF)
                if self.index < 3:
                    buffer[chip, half, 0] = high[here]
                    buffer[chip, half, 1] = low[here]
                else:
                    buffer[chip, half] = high[here]
            for d in (1, 3, 2):
                self.send(0, 0, 0, d, 0)
                self.send(0, 0, 1, 0, d)
            for d in (2, 1, 3):
                self.send(0, 0, 0, 0, d)
                self.send(0, 0, 1, d, 0)

        def forward(self):
            half_block = self.buffer.at[0, 0]
            for d in (1, 3, 2):
                self.arrive(d, half_block)
                for e in (2, 1, 3):
                    self.send(d, 0, 0, 0, e)
                self.arrive(3 + d, half_block)
                for e in (2, 1, 3):
                    self.send(0, d, 1, e, 0)

        def near(self):
            self.arrive(7, self.buffer.at[pl.ds(0, 3)])

        def middle(self):
            self.arrive(8, self.buffer.at[pl.ds(0, 4)])

        def far(self):
            self.arrive(0, self.buffer.at[pl.ds(0, 5)])

    def multiply(buffer, planes, blocks):
        places = [at(x + dx, y + dy) for dx, dy in blocks]
        left = jnp.concatenate([buffer[i].reshape(planes * MINE, WIDE) for i in places], axis=1)
        right = jnp.concatenate([matrix[i].reshape(2 * WIDE, WIDE) for i in places], axis=1)
        return lax.dot_general(left, right, (((1,), (1,)), ((), ())), preferred_element_type=F32)

    def fold(total, planes):
        if planes == 2:
            total = total.reshape(2, 2, HALF, 2 * WIDE)
            total = (total[:, 0] + total[:, 1]).reshape(MINE, 2 * WIDE)
        return jnp.concatenate(
            [total[:, i * WIDE : i * WIDE + ROWS] + total[:, i * WIDE + ROWS : (i + 1) * WIDE] for i in (0, 1)],
            axis=1,
        )

    def whole(buffer, planes, origin):
        block = buffer[origin].astype(F32)
        if planes == 2:
            block = block[:, 0] + block[:, 1]
        return block.reshape(MINE, WIDE)

    def products(gather, planes, blocks, first_time):
        for dx, dy in blocks:
            origin = at(x + dx, y + dy)
            block = whole(gather.buffer, planes, origin)
            if first_time:
                residual[origin] = block
                terms = block * block
            else:
                terms = residual[origin] * block
            dots[origin] = terms[:, :ROWS] + terms[:, ROWS:]
        return multiply(gather.buffer, planes, blocks)

    def finish(gather, planes, first_time=False):
        gather.forward()
        gather.near()
        height = planes * MINE
        product[:height] = products(gather, planes, near_blocks, first_time)
        gather.middle()
        product[:height] = product[:height] + products(gather, planes, middle_blocks, first_time)
        gather.far()
        total = product[:height] + products(gather, planes, far_blocks, first_time)
        return fold(total, planes), column_sum(jnp.sum(dots[...], axis=0))

    zero = jnp.zeros((MINE, WIDE), F32)

    gather = Gather(0, gather_b)
    gather.start(own_r)
    await_bytes(matrix.at[:, other], matrix_sem)
    own_w, norm = finish(gather, 2, True)
    initial = norm

    alpha = beta = None
    own_p = own_s = own_t = own_x = None
    for step, (buffer, planes) in enumerate(((gather_0, 2), (gather_1, 2), (gather_2, 1))):
        gather = Gather(step + 1, buffer)
        gather.start(own_w)
        if step > 0:
            before, before_planes = ((gather_0, 2), (gather_1, 2))[step - 1]

            def advance(origin, total, buffer=before, planes=before_planes, step=step, alpha=alpha, beta=old_beta):
                direction = whole(buffer, planes, origin)
                if step > 1:
                    direction = direction + beta * mapped_dir[origin]
                mapped_dir[origin] = direction
                block = residual[origin] - alpha * direction
                residual[origin] = block
                return total + block * block

            following = column_sum(lax.fori_loop(0, CHIPS, advance, zero))
            beta = following / norm
            norm = following
        own_u, overlap = finish(gather, planes)
        if step == 0:
            alpha = norm / overlap
            own_p, own_s, own_t = own_r, own_w, own_u
            own_x = alpha * own_p
        else:
            alpha = norm / (overlap - beta * norm / alpha)
            own_p = own_r + beta * own_p
            own_s = own_w + beta * own_s
            own_t = own_u + beta * own_t
            own_x = own_x + alpha * own_p
        old_beta = beta
        own_r = own_r - alpha * own_s
        own_w = own_w - alpha * own_t

    def last_advance(origin, total):
        direction = whole(gather_2, 1, origin) + beta * mapped_dir[origin]
        block = residual[origin] - alpha * direction
        return total + block * block

    following = column_sum(lax.fori_loop(0, CHIPS, last_advance, zero))
    beta = following / norm
    norm = following

    own_s = own_w + beta * own_s
    own_p = own_r + beta * own_p
    close = own_r - alpha * own_s
    lane = lax.broadcasted_iota(jnp.int32, (MINE, ROWS), 1)
    packed = jnp.zeros((MINE, ROWS), F32)
    for i, terms in enumerate((own_r * own_w, close * close, close * own_s, own_s * own_s)):
        packed = jnp.where(lane == i, column_sum(terms), packed)
    packed = jnp.transpose(jnp.concatenate([packed, jnp.zeros_like(packed)], axis=0))
    sums[chip] = packed[:8]

    def tell_chip(n, _):
        push(sums.at[chip], sums.at[chip], send_sem.at[8], sums_sem, device(lax.rem(chip + n, CHIPS)))
        return 0

    lax.fori_loop(1, CHIPS, tell_chip, 0)
    await_bytes(sums.at[pl.ds(0, CHIPS - 1)], sums_sem)
    gathered = jnp.sum(sums[...], axis=0)
    gathered = jnp.transpose(jnp.concatenate([gathered, jnp.zeros((ROWS - 8, ROWS), F32)], axis=0))[:MINE]
    overlap, close_close, close_s, s_s = (gathered[:, i : i + 1] for i in range(4))
    last = norm / (overlap - beta * norm / alpha)
    excess = last - alpha
    final = jnp.maximum(close_close - 2.0 * excess * close_s + excess * excess * s_s, 0.0)

    place = grp * 2 + core
    both = jnp.where(lane == 0, final, jnp.where(lane == 1, initial, 0.0))
    totals[place] = jnp.sum(both, axis=0, keepdims=True)

    def tell_group(n, _):
        there = lax.rem(place + n, 2 * groups)
        push(
            totals.at[place], totals.at[place], send_sem.at[10], totals_sem,
            (lax.div(there, 2), chip * 2 + lax.rem(there, 2)),
        )
        return 0

    lax.fori_loop(1, 2 * groups, tell_group, 0)
    own_x = own_x + last * own_p
    answer[core, 0] = own_x[:, :ROWS]
    answer[core, 1] = own_x[:, ROWS:]
    push(answer.at[core, other], answer.at[core, other], send_sem.at[9], answer_sem, partner)
    await_bytes(answer.at[other, core], answer_sem)
    merged_out[...] = jnp.transpose(jnp.concatenate([answer[0, core], answer[1, core]], axis=0))
    merged_copy = pltpu.make_async_copy(merged_out, merged, local_sem.at[1])
    merged_copy.start()

    await_bytes(partner_part, send_sem.at[0])
    await_bytes(matrix.at[:, 0], send_sem.at[1])
    await_bytes(first.at[:, pl.ds(0, 3)], send_sem.at[2])
    await_bytes(second.at[:, 0, pl.ds(0, 3)], send_sem.at[3])
    for i, buffer in enumerate((gather_b, gather_0, gather_1, gather_2)):
        await_bytes(buffer.at[pl.ds(0, CHIPS - 1)], send_sem.at[4 + i])
    await_bytes(sums.at[pl.ds(0, CHIPS - 1)], send_sem.at[8])
    await_bytes(answer.at[0, 0], send_sem.at[9])
    await_bytes(totals.at[pl.ds(0, 2 * groups - 1)], send_sem.at[10])
    merged_copy.wait()
    await_bytes(totals.at[pl.ds(0, 2 * groups - 1)], totals_sem)
    over_all = jnp.sum(totals[...], axis=0)
    ratio_out[...] = jnp.sqrt(over_all[:, 0:1] / over_all[:, 1:2]) + jnp.zeros((1, ROWS), F32)
    ratio_copy = pltpu.make_async_copy(ratio_out, ratio, local_sem.at[0])
    ratio_copy.start()
    ratio_copy.wait()


def local(expert_grams, expert_weights):
    groups = lax.axis_size("grp")
    hbm = pl.BlockSpec(memory_space=pltpu.HBM)
    anywhere = pl.BlockSpec(memory_space=pl.ANY)
    dma = pltpu.SemaphoreType.DMA
    merged, ratio = pl.pallas_call(
        kernel,
        out_shape=(jax.ShapeDtypeStruct((ROWS, COLS), F32), jax.ShapeDtypeStruct((1, ROWS), F32)),
        in_specs=[hbm, hbm],
        out_specs=(anywhere, anywhere),
        scratch_shapes=[
            pltpu.VMEM((CHIPS, EXPERTS, ROWS, WIDE), F32),
            pltpu.VMEM((CHIPS, 2, 2, ROWS, WIDE), BF16),
            pltpu.VMEM((EXPERTS, ROWS, COLS), BF16),
            pltpu.VMEM((COLS, 2 * EXPERTS * ROWS), BF16),
            pltpu.VMEM((CHIPS, 2, MINE, WIDE), F32),
            pltpu.VMEM((CHIPS, MINE, WIDE), F32),
            pltpu.VMEM((2, SIDE, SIDE, HALF, WIDE), F32),
            pltpu.VMEM((2, 2, SIDE, HALF, WIDE), F32),
            pltpu.VMEM((CHIPS, MINE, WIDE), F32),
            pltpu.VMEM((CHIPS, 2, 2, HALF, WIDE), BF16),
            pltpu.VMEM((CHIPS, 2, 2, HALF, WIDE), BF16),
            pltpu.VMEM((CHIPS, 2, 2, HALF, WIDE), BF16),
            pltpu.VMEM((CHIPS, 2, HALF, WIDE), BF16),
            pltpu.VMEM((CHIPS, MINE, WIDE), F32),
            pltpu.VMEM((CHIPS, MINE, WIDE), F32),
            pltpu.VMEM((CHIPS, MINE, ROWS), F32),
            pltpu.VMEM((2 * MINE, 2 * WIDE), F32),
            pltpu.VMEM((CHIPS, 8, ROWS), F32),
            pltpu.VMEM((2 * groups, 1, ROWS), F32),
            pltpu.VMEM((2, 2, MINE, ROWS), F32),
            pltpu.VMEM((ROWS, COLS), F32),
            pltpu.VMEM((1, ROWS), F32),
            dma((CHIPS,)),
            dma((CHIPS,)),
            dma,
            dma((2, SIDE, SIDE)),
            dma((2, SIDE)),
            dma((4, 9)),
            dma,
            dma,
            dma,
            dma((11,)),
            dma((2,)),
        ],
        compiler_params=pltpu.CompilerParams(
            collective_id=0, has_side_effects=True, vmem_limit_bytes=55040 * 1024
        ),
        name="merge",
    )(expert_grams, expert_weights)
    return merged, ratio[0, 0]


def solution(mesh):
    placed = (P(None, "row", None), P(None, "row", "grp"))
    return jax.shard_map(
        local, mesh=mesh, in_specs=placed, out_specs=(P("row", "grp"), P()), check_vma=False
    )
```

time: 89.6 us -> 78.9 us (0.88)
  Pallas kernels: 85.6 us -> 76.4 us
    pallas_call x1, Pallas kernels: 85.6 us -> 76.4 us  [local(): pl.pallas_call(kernel, out_shape=(jax.ShapeDtypeStruct((ROWS, COLS), F32)...]
where the time goes in v2:
time: 78.9 us; the launch traced here: 78.8 us
  Pallas kernels  76.4 us (97%)
  between operations  1.8 us (2%)
    pallas_call x1, Pallas kernels, local(): pl.pallas_call(kernel, out_shape=(jax.ShapeDtypeStruct((ROWS, COLS), F32)...  76.4 us

profile of v2, /device:TPU:1, one launch (start us, length us, event | category | flops | bytes accessed | tf_op | source)
XLA Modules:
  0.0 78.8 jit_solution(16740524545761971521)
XLA Ops:
  0.6 76.4 %merge.1 = (f32[128,128]{1,0:T(8,128)S(1)}, f32[1,128]{1,0:T(1,128)S(1)}) custom-call(f32[4,128,4096]{2,1,0:T(8,128)} %grams.1, bf16[4,128,128]{2,1,0:T(8,128)(2,1)} %weights.1), custom_call_target="tpu_custom_call" | custom-call | tf_op jit(solution)/shard_map/merge/pallas_call | solution.py:387
  77.0 0.6 copy.6

commit v3 on v2

--- a/solution.py
+++ b/solution.py
@@ -9,6 +9,7 @@
 F32, BF16 = jnp.float32, jnp.bfloat16
 EXPERTS, ROWS, COLS = 4, 128, 128
 CHIPS, SIDE, WIDE, MINE, HALF = 16, 4, 256, 64, 32
+GROUP = 4
 
 
 def split(x):
@@ -26,7 +27,7 @@
     gather_b, gather_0, gather_1, gather_2, residual, mapped_dir, dots, product,
     sums, totals, answer, merged_out, ratio_out,
     panel_sem, partner_sem, matrix_sem, first_sem, second_sem, gather_sem, sums_sem, totals_sem, answer_sem,
-    send_sem, local_sem,
+    send_sem, local_sem, token_sem,
 ):
     grp, row = lax.axis_index("grp"), lax.axis_index("row")
     core, chip = lax.rem(row, 2), lax.div(row, 2)
@@ -47,6 +48,13 @@
     def await_bytes(ref, sem):
         pltpu.make_async_copy(ref, ref, sem).wait()
 
+    groups = lax.axis_size("grp")
+    barrier = pltpu.get_barrier_semaphore()
+    along_z = [(lax.rem(grp + d, groups), row) for d in (2, groups - 2, 1, groups - 1)]
+    lines = [device(at(x + d, y)) for d in (2, 1, 3)] + [device(at(x, y + d)) for d in (2, 1, 3)]
+    for there in (*along_z, *lines, partner):
+        pl.semaphore_signal(barrier, 1, device_id=there, device_id_type=MESH)
+
     weights_copy = pltpu.make_async_copy(weights, weights_in, local_sem.at[0])
     weights_copy.start()
 
@@ -60,23 +68,12 @@
 
     lax.fori_loop(0, CHIPS, fetch, 0)
 
-    barrier = pltpu.get_barrier_semaphore()
-
-    def greet_chip(n, _):
-        pl.semaphore_signal(barrier, 1, device_id=device(lax.rem(chip + n, CHIPS)), device_id_type=MESH)
-        return 0
-
-    lax.fori_loop(1, CHIPS, greet_chip, 0)
-    groups = lax.axis_size("grp")
-
-    def greet_group(n, _):
-        there = lax.rem(grp * 2 + core + n, 2 * groups)
-        pl.semaphore_signal(
-            barrier, 1, device_id=(lax.div(there, 2), chip * 2 + lax.rem(there, 2)), device_id_type=MESH
-        )
-        return 0
-
-    lax.fori_loop(1, 2 * groups, greet_group, 0)
+    def tell_z(i):
+        for there in along_z:
+            pl.semaphore_signal(token_sem.at[i], 1, device_id=there, device_id_type=MESH)
+
+    def hear_z(i):
+        pl.semaphore_wait(token_sem.at[i], len(along_z))
 
     weights_copy.wait()
     turned = jnp.transpose(weights_in[...].reshape(EXPERTS * ROWS, COLS).astype(F32)).astype(BF16)
@@ -84,25 +81,31 @@
     weights_t[:, EXPERTS * ROWS :] = turned
 
     def compute_panel(target):
-        panel_copy(target).wait()
         high, low = split(panel[target].reshape(EXPERTS * ROWS, WIDE))
         product = jnp.dot(weights_t[...], jnp.concatenate([high, low], axis=0), preferred_element_type=F32)
         partial[target] = product.reshape(2, MINE, WIDE)
         system = (panel[target, 0] + panel[target, 1]) + (panel[target, 2] + panel[target, 3])
-        rows = lax.broadcasted_iota(jnp.int32, (ROWS, WIDE), 0) + (chip * WIDE + core * ROWS)
-        columns = lax.broadcasted_iota(jnp.int32, (ROWS, WIDE), 1) + target * WIDE
-        system_high, system_low = split(system + (rows == columns).astype(F32))
+        system_high, system_low = split(system)
         matrix[target, core, 0] = system_high
         matrix[target, core, 1] = system_low
 
     def panel_step(n, _):
-        for i in range(4):
-            compute_panel(4 * n + i)
+        for i in range(GROUP):
+            panel_copy(GROUP * n + i).wait()
+        for i in range(GROUP):
+            compute_panel(GROUP * n + i)
         return 0
 
-    lax.fori_loop(0, CHIPS // 4, panel_step, 0)
-
-    pl.semaphore_wait(barrier, CHIPS - 1 + 2 * groups - 1)
+    lax.fori_loop(0, CHIPS // GROUP, panel_step, 0)
+
+    system = (panel[chip, 0] + panel[chip, 1]) + (panel[chip, 2] + panel[chip, 3])
+    below = lax.broadcasted_iota(jnp.int32, (ROWS, WIDE), 0) + core * ROWS
+    system = system + (below == lax.broadcasted_iota(jnp.int32, (ROWS, WIDE), 1)).astype(F32)
+    system_high, system_low = split(system)
+    matrix[chip, core, 0] = system_high
+    matrix[chip, core, 1] = system_low
+
+    pl.semaphore_wait(barrier, len(along_z) + len(lines) + 1)
 
     targets = [(2, 2), (1, 2), (3, 2), (2, 1), (2, 3), (1, 1), (3, 1), (1, 3), (3, 3)]
     targets += [(0, 2), (2, 0), (0, 1), (1, 0), (0, 3), (3, 0), (0, 0)]
@@ -135,6 +138,8 @@
             total = total + first[half, source, place]
         return total, target
 
+    tell_z(0)
+
     for k in (2, 1, 3):
         for half in (0, 1):
             along = y if half == 0 else x
@@ -163,11 +168,11 @@
 
     near_blocks = [(0, 0), (1, 0), (3, 0), (0, 1), (0, 3), (2, 0), (0, 2)]
     middle_blocks = [(1, 1), (1, 3), (3, 1), (3, 3)]
-    far_blocks = [(2, 1), (2, 3), (1, 2), (3, 2), (2, 2)]
+    far_blocks = [(2, 1), (2, 3), (1, 2), (3, 2)]
 
     def place_of(dx, dy, half):
         if dx != 0 and dy != 0:
-            return 0 if 2 in (dx, dy) else 8
+            return 9 if (dx, dy) == (2, 2) else 0 if 2 in (dx, dy) else 8
         if half == 0:
             return dx if dy == 0 else 7
         return 3 + dy if dx == 0 else 7
@@ -194,9 +199,11 @@
                     buffer[chip, half, 1] = low[here]
                 else:
                     buffer[chip, half] = high[here]
-            for d in (1, 3, 2):
+            for d in (2, 1, 3):
                 self.send(0, 0, 0, d, 0)
                 self.send(0, 0, 1, 0, d)
+
+        def start_rest(self):
             for d in (2, 1, 3):
                 self.send(0, 0, 0, 0, d)
                 self.send(0, 0, 1, d, 0)
@@ -218,7 +225,10 @@
             self.arrive(8, self.buffer.at[pl.ds(0, 4)])
 
         def far(self):
-            self.arrive(0, self.buffer.at[pl.ds(0, 5)])
+            self.arrive(0, self.buffer.at[pl.ds(0, 4)])
+
+        def last(self):
+            self.arrive(9, self.buffer.at[0])
 
     def multiply(buffer, planes, blocks):
         places = [at(x + dx, y + dy) for dx, dy in blocks]
@@ -261,14 +271,19 @@
         gather.middle()
         product[:height] = product[:height] + products(gather, planes, middle_blocks, first_time)
         gather.far()
-        total = product[:height] + products(gather, planes, far_blocks, first_time)
+        product[:height] = product[:height] + products(gather, planes, far_blocks, first_time)
+        gather.last()
+        total = product[:height] + products(gather, planes, [(2, 2)], first_time)
         return fold(total, planes), column_sum(jnp.sum(dots[...], axis=0))
 
     zero = jnp.zeros((MINE, WIDE), F32)
 
     gather = Gather(0, gather_b)
     gather.start(own_r)
+    hear_z(0)
+    tell_z(1)
     await_bytes(matrix.at[:, other], matrix_sem)
+    gather.start_rest()
     own_w, norm = finish(gather, 2, True)
     initial = norm
 
@@ -292,6 +307,7 @@
             following = column_sum(lax.fori_loop(0, CHIPS, advance, zero))
             beta = following / norm
             norm = following
+        gather.start_rest()
         own_u, overlap = finish(gather, planes)
         if step == 0:
             alpha = norm / overlap
@@ -320,28 +336,34 @@
     own_p = own_r + beta * own_p
     close = own_r - alpha * own_s
     lane = lax.broadcasted_iota(jnp.int32, (MINE, ROWS), 1)
-    packed = jnp.zeros((MINE, ROWS), F32)
-    for i, terms in enumerate((own_r * own_w, close * close, close * own_s, own_s * own_s)):
-        packed = jnp.where(lane == i, column_sum(terms), packed)
-    packed = jnp.transpose(jnp.concatenate([packed, jnp.zeros_like(packed)], axis=0))
-    sums[chip] = packed[:8]
+    def lay_flat(columns):
+        packed = jnp.zeros((MINE, ROWS), F32)
+        for i, column in enumerate(columns):
+            packed = jnp.where(lane == i, column, packed)
+        return jnp.transpose(jnp.concatenate([packed, jnp.zeros_like(packed)], axis=0))[: len(columns)]
+
+    sums[chip] = lay_flat([column_sum(t) for t in (own_r * own_w, close * close, close * own_s, own_s * own_s)])
 
     def tell_chip(n, _):
         push(sums.at[chip], sums.at[chip], send_sem.at[8], sums_sem, device(lax.rem(chip + n, CHIPS)))
         return 0
 
     lax.fori_loop(1, CHIPS, tell_chip, 0)
+    hear_z(1)
+    known = lay_flat([norm, beta, alpha, initial])
+    used = lax.broadcasted_iota(jnp.int32, (1, ROWS), 1) < MINE
+    norm, beta, alpha, initial = (jnp.where(used, known[i : i + 1], 1.0) for i in range(4))
     await_bytes(sums.at[pl.ds(0, CHIPS - 1)], sums_sem)
-    gathered = jnp.sum(sums[...], axis=0)
-    gathered = jnp.transpose(jnp.concatenate([gathered, jnp.zeros((ROWS - 8, ROWS), F32)], axis=0))[:MINE]
-    overlap, close_close, close_s, s_s = (gathered[:, i : i + 1] for i in range(4))
-    last = norm / (overlap - beta * norm / alpha)
+    gathered = jnp.where(used, jnp.sum(sums[...], axis=0), 1.0)
+    overlap, close_close, close_s, s_s = (gathered[i : i + 1] for i in range(4))
+    last = norm / jnp.where(used, overlap - beta * norm / alpha, 1.0)
     excess = last - alpha
     final = jnp.maximum(close_close - 2.0 * excess * close_s + excess * excess * s_s, 0.0)
 
     place = grp * 2 + core
-    both = jnp.where(lane == 0, final, jnp.where(lane == 1, initial, 0.0))
-    totals[place] = jnp.sum(both, axis=0, keepdims=True)
+    final = column_sum(jnp.where(used, final, 0.0))
+    initial = column_sum(jnp.where(used, initial, 0.0))
+    totals[place] = jnp.where(lax.broadcasted_iota(jnp.int32, (1, ROWS), 1) == 0, final, initial)
 
     def tell_group(n, _):
         there = lax.rem(place + n, 2 * groups)
@@ -352,6 +374,7 @@
         return 0
 
     lax.fori_loop(1, 2 * groups, tell_group, 0)
+    last = jnp.transpose(jnp.broadcast_to(last, (ROWS, ROWS)))[:MINE, :1]
     own_x = own_x + last * own_p
     answer[core, 0] = own_x[:, :ROWS]
     answer[core, 1] = own_x[:, ROWS:]
@@ -407,7 +430,7 @@
             pltpu.VMEM((CHIPS, MINE, WIDE), F32),
             pltpu.VMEM((CHIPS, MINE, ROWS), F32),
             pltpu.VMEM((2 * MINE, 2 * WIDE), F32),
-            pltpu.VMEM((CHIPS, 8, ROWS), F32),
+            pltpu.VMEM((CHIPS, 4, ROWS), F32),
             pltpu.VMEM((2 * groups, 1, ROWS), F32),
             pltpu.VMEM((2, 2, MINE, ROWS), F32),
             pltpu.VMEM((ROWS, COLS), F32),
@@ -417,12 +440,13 @@
             dma,
             dma((2, SIDE, SIDE)),
             dma((2, SIDE)),
-            dma((4, 9)),
+            dma((4, 10)),
             dma,
             dma,
             dma,
             dma((11,)),
             dma((2,)),
+            pltpu.SemaphoreType.REGULAR((2,)),
         ],
         compiler_params=pltpu.CompilerParams(
             collective_id=0, has_side_effects=True, vmem_limit_bytes=55040 * 1024

time: 78.9 us -> 76.8 us (0.973)
  Pallas kernels: 76.4 us -> 74.3 us
    pallas_call x1, Pallas kernels: 76.4 us -> 74.3 us  [local(): pl.pallas_call(kernel, out_shape=(jax.ShapeDtypeStruct((ROWS, COLS), F32)...]
where the time goes in v3:
time: 76.8 us; the launch traced here: 76.7 us
  Pallas kernels  74.3 us (97%)
  between operations  1.8 us (2%)
    pallas_call x1, Pallas kernels, local(): pl.pallas_call(kernel, out_shape=(jax.ShapeDtypeStruct((ROWS, COLS), F32)...  74.3 us

profile of v3, /device:TPU:1, one launch (start us, length us, event | category | flops | bytes accessed | tf_op | source)
XLA Modules:
  0.0 76.7 jit_solution(6893490772382950573)
XLA Ops:
  0.6 74.3 %merge.1 = (f32[128,128]{1,0:T(8,128)S(1)}, f32[1,128]{1,0:T(1,128)S(1)}) custom-call(f32[4,128,4096]{2,1,0:T(8,128)} %grams.1, bf16[4,128,128]{2,1,0:T(8,128)(2,1)} %weights.1), custom_call_target="tpu_custom_call" | custom-call | tf_op jit(solution)/shard_map/merge/pallas_call | solution.py:410
  74.9 0.6 copy.6

commit v4 on v3

--- a/solution.py
+++ b/solution.py
@@ -9,7 +9,7 @@
 F32, BF16 = jnp.float32, jnp.bfloat16
 EXPERTS, ROWS, COLS = 4, 128, 128
 CHIPS, SIDE, WIDE, MINE, HALF = 16, 4, 256, 64, 32
-GROUP = 4
+GROUP, BEFORE = 4, 0
 
 
 def split(x):
@@ -52,21 +52,22 @@
     barrier = pltpu.get_barrier_semaphore()
     along_z = [(lax.rem(grp + d, groups), row) for d in (2, groups - 2, 1, groups - 1)]
     lines = [device(at(x + d, y)) for d in (2, 1, 3)] + [device(at(x, y + d)) for d in (2, 1, 3)]
+    order = [(2, 2), (1, 2), (3, 2), (2, 1), (2, 3), (1, 1), (3, 1), (1, 3), (3, 3)]
+    order += [(0, 2), (2, 0), (0, 1), (1, 0), (0, 3), (3, 0), (0, 0)]
+    targets = [at(x + dx, y + dy) for dx, dy in order]
+
+    def panel_copy(n):
+        columns = pl.ds(pl.multiple_of(targets[n] * WIDE, WIDE), WIDE)
+        return pltpu.make_async_copy(grams.at[:, :, columns], panel.at[n], panel_sem.at[n])
+
+    weights_copy = pltpu.make_async_copy(weights, weights_in, local_sem.at[0])
+    weights_copy.start()
+    for n in range(GROUP):
+        panel_copy(n).start()
     for there in (*along_z, *lines, partner):
         pl.semaphore_signal(barrier, 1, device_id=there, device_id_type=MESH)
-
-    weights_copy = pltpu.make_async_copy(weights, weights_in, local_sem.at[0])
-    weights_copy.start()
-
-    def panel_copy(n):
-        columns = pl.ds(pl.multiple_of(n * WIDE, WIDE), WIDE)
-        return pltpu.make_async_copy(grams.at[:, :, columns], panel.at[n], panel_sem.at[n])
-
-    def fetch(n, _):
+    for n in range(GROUP, CHIPS):
         panel_copy(n).start()
-        return 0
-
-    lax.fori_loop(0, CHIPS, fetch, 0)
 
     def tell_z(i):
         for there in along_z:
@@ -80,40 +81,25 @@
     weights_t[:, : EXPERTS * ROWS] = turned
     weights_t[:, EXPERTS * ROWS :] = turned
 
-    def compute_panel(target):
-        high, low = split(panel[target].reshape(EXPERTS * ROWS, WIDE))
+    def compute_panel(n):
+        target = targets[n]
+        high, low = split(panel[n].reshape(EXPERTS * ROWS, WIDE))
         product = jnp.dot(weights_t[...], jnp.concatenate([high, low], axis=0), preferred_element_type=F32)
         partial[target] = product.reshape(2, MINE, WIDE)
-        system = (panel[target, 0] + panel[target, 1]) + (panel[target, 2] + panel[target, 3])
+        system = (panel[n, 0] + panel[n, 1]) + (panel[n, 2] + panel[n, 3])
+        if order[n] == (0, 0):
+            below = lax.broadcasted_iota(jnp.int32, (ROWS, WIDE), 0) + core * ROWS
+            system = system + (below == lax.broadcasted_iota(jnp.int32, (ROWS, WIDE), 1)).astype(F32)
         system_high, system_low = split(system)
         matrix[target, core, 0] = system_high
         matrix[target, core, 1] = system_low
 
-    def panel_step(n, _):
-        for i in range(GROUP):
-            panel_copy(GROUP * n + i).wait()
-        for i in range(GROUP):
-            compute_panel(GROUP * n + i)
-        return 0
-
-    lax.fori_loop(0, CHIPS // GROUP, panel_step, 0)
-
-    system = (panel[chip, 0] + panel[chip, 1]) + (panel[chip, 2] + panel[chip, 3])
-    below = lax.broadcasted_iota(jnp.int32, (ROWS, WIDE), 0) + core * ROWS
-    system = system + (below == lax.broadcasted_iota(jnp.int32, (ROWS, WIDE), 1)).astype(F32)
-    system_high, system_low = split(system)
-    matrix[chip, core, 0] = system_high
-    matrix[chip, core, 1] = system_low
-
-    pl.semaphore_wait(barrier, len(along_z) + len(lines) + 1)
-
-    targets = [(2, 2), (1, 2), (3, 2), (2, 1), (2, 3), (1, 1), (3, 1), (1, 3), (3, 3)]
-    targets += [(0, 2), (2, 0), (0, 1), (1, 0), (0, 3), (3, 0), (0, 0)]
-    for dx, dy in targets:
-        target = at(x + dx, y + dy)
+    def swap_panel(n):
+        target = targets[n]
         push(partial.at[target, other], partner_part.at[target], send_sem.at[0], partner_sem.at[target], partner)
-    for dx, dy in targets:
-        target = at(x + dx, y + dy)
+
+    def forward_panel(n):
+        (dx, dy), target = order[n], targets[n]
         await_bytes(partner_part.at[target], partner_sem.at[target])
         outgoing[target] = partial[target, core] + partner_part[target]
         if dx != 0:
@@ -126,6 +112,30 @@
                 outgoing.at[target, pl.ds(HALF, HALF)], first.at[1, y, lax.rem(x + dx, SIDE)],
                 send_sem.at[2], first_sem.at[1, y, lax.rem(x + dx, SIDE)], device(at(x, y + dy)),
             )
+
+    def compute_group(group):
+        for n in group:
+            panel_copy(n).wait()
+        for n in group:
+            compute_panel(n)
+
+    groups_of_panels = [range(i, i + GROUP) for i in range(0, CHIPS, GROUP)]
+    for i, group in enumerate(groups_of_panels):
+        compute_group(group)
+        if i == BEFORE:
+            pl.semaphore_wait(barrier, len(along_z) + len(lines) + 1)
+            for earlier in groups_of_panels[:BEFORE]:
+                for n in earlier:
+                    swap_panel(n)
+        if i >= BEFORE:
+            for n in group:
+                swap_panel(n)
+        if i > BEFORE:
+            for n in groups_of_panels[i - BEFORE - 1]:
+                forward_panel(n)
+    for group in groups_of_panels[len(groups_of_panels) - BEFORE - 1 :]:
+        for n in group:
+            forward_panel(n)
 
     def first_sum(half, k):
         line, along = (x, y) if half == 0 else (y, x)

time: 76.8 us -> 74.4 us (0.969)
  Pallas kernels: 74.3 us -> 71.9 us
    pallas_call x1, Pallas kernels: 74.3 us -> 71.9 us  [local(): pl.pallas_call(kernel, out_shape=(jax.ShapeDtypeStruct((ROWS, COLS), F32)...]
where the time goes in v4:
time: 74.4 us; the launch traced here: 74.3 us
  Pallas kernels  71.9 us (97%)
  between operations  1.8 us (2%)
    pallas_call x1, Pallas kernels, local(): pl.pallas_call(kernel, out_shape=(jax.ShapeDtypeStruct((ROWS, COLS), F32)...  71.9 us

profile of v4, /device:TPU:1, one launch (start us, length us, event | category | flops | bytes accessed | tf_op | source)
XLA Modules:
  0.0 74.3 jit_solution(12384529970260222253)
XLA Ops:
  0.6 71.9 %merge.1 = (f32[128,128]{1,0:T(8,128)S(1)}, f32[1,128]{1,0:T(1,128)S(1)}) custom-call(f32[4,128,4096]{2,1,0:T(8,128)} %grams.1, bf16[4,128,128]{2,1,0:T(8,128)(2,1)} %weights.1), custom_call_target="tpu_custom_call" | custom-call | tf_op jit(solution)/shard_map/merge/pallas_call | solution.py:420
  72.5 0.6 copy.6

commit v5 on v4

--- a/solution.py
+++ b/solution.py
@@ -9,7 +9,7 @@
 F32, BF16 = jnp.float32, jnp.bfloat16
 EXPERTS, ROWS, COLS = 4, 128, 128
 CHIPS, SIDE, WIDE, MINE, HALF = 16, 4, 256, 64, 32
-GROUP, BEFORE = 4, 0
+GROUP, BEFORE = 2, 0
 
 
 def split(x):
@@ -25,7 +25,7 @@
     grams, weights, merged, ratio,
     panel, matrix, weights_in, weights_t, partial, partner_part, first, second, outgoing,
     gather_b, gather_0, gather_1, gather_2, residual, mapped_dir, dots, product,
-    sums, totals, answer, merged_out, ratio_out,
+    sums, totals, answer,
     panel_sem, partner_sem, matrix_sem, first_sem, second_sem, gather_sem, sums_sem, totals_sem, answer_sem,
     send_sem, local_sem, token_sem,
 ):
@@ -58,7 +58,7 @@
 
     def panel_copy(n):
         columns = pl.ds(pl.multiple_of(targets[n] * WIDE, WIDE), WIDE)
-        return pltpu.make_async_copy(grams.at[:, :, columns], panel.at[n], panel_sem.at[n])
+        return pltpu.make_async_copy(grams.at[:, :, columns], panel.at[n], panel_sem.at[n // GROUP])
 
     weights_copy = pltpu.make_async_copy(weights, weights_in, local_sem.at[0])
     weights_copy.start()
@@ -96,26 +96,26 @@
 
     def swap_panel(n):
         target = targets[n]
-        push(partial.at[target, other], partner_part.at[target], send_sem.at[0], partner_sem.at[target], partner)
+        push(partial.at[target, other], partner_part.at[target], send_sem.at[0], partner_sem.at[n // GROUP], partner)
 
     def forward_panel(n):
         (dx, dy), target = order[n], targets[n]
-        await_bytes(partner_part.at[target], partner_sem.at[target])
+        if n % GROUP == 0:
+            await_bytes(partner_part.at[pl.ds(0, GROUP)], partner_sem.at[n // GROUP])
         outgoing[target] = partial[target, core] + partner_part[target]
         if dx != 0:
             push(
                 outgoing.at[target, pl.ds(0, HALF)], first.at[0, x, lax.rem(y + dy, SIDE)],
-                send_sem.at[2], first_sem.at[0, x, lax.rem(y + dy, SIDE)], device(at(x + dx, y)),
+                send_sem.at[2], first_sem.at[0, lax.rem(y + dy, SIDE)], device(at(x + dx, y)),
             )
         if dy != 0:
             push(
                 outgoing.at[target, pl.ds(HALF, HALF)], first.at[1, y, lax.rem(x + dx, SIDE)],
-                send_sem.at[2], first_sem.at[1, y, lax.rem(x + dx, SIDE)], device(at(x, y + dy)),
+                send_sem.at[2], first_sem.at[1, lax.rem(x + dx, SIDE)], device(at(x, y + dy)),
             )
 
     def compute_group(group):
-        for n in group:
-            panel_copy(n).wait()
+        await_bytes(panel.at[pl.ds(0, GROUP)], panel_sem.at[group[0] // GROUP])
         for n in group:
             compute_panel(n)
 
@@ -142,10 +142,9 @@
         place = lax.rem(along + k, SIDE)
         target = at(x, place) if half == 0 else at(place, y)
         total = outgoing[target, pl.ds(half * HALF, HALF)]
+        await_bytes(first.at[half, pl.ds(0, SIDE - 1), 0], first_sem.at[half, place])
         for j in (1, 3, 2):
-            source = lax.rem(line + j, SIDE)
-            await_bytes(first.at[half, source, place], first_sem.at[half, source, place])
-            total = total + first[half, source, place]
+            total = total + first[half, lax.rem(line + j, SIDE), place]
         return total, target
 
     tell_z(0)
@@ -157,7 +156,7 @@
             second[half, 0, k] = total
             push(
                 second.at[half, 0, k], second.at[half, 1, along],
-                send_sem.at[3], second_sem.at[half, along], device(target),
+                send_sem.at[3], second_sem.at[half], device(target),
             )
     def send_matrix(target, _):
         push(matrix.at[target, core], matrix.at[target, core], send_sem.at[1], matrix_sem, partner)
@@ -169,10 +168,9 @@
     for half in (0, 1):
         along = y if half == 0 else x
         total, _ = first_sum(half, 0)
+        await_bytes(second.at[half, 1, pl.ds(0, SIDE - 1)], second_sem.at[half])
         for j in (1, 3, 2):
-            source = lax.rem(along + j, SIDE)
-            await_bytes(second.at[half, 1, source], second_sem.at[half, source])
-            total = total + second[half, 1, source]
+            total = total + second[half, 1, lax.rem(along + j, SIDE)]
         pieces.append(total)
     own_r = jnp.concatenate(pieces, axis=0)
 
@@ -390,9 +388,7 @@
     answer[core, 1] = own_x[:, ROWS:]
     push(answer.at[core, other], answer.at[core, other], send_sem.at[9], answer_sem, partner)
     await_bytes(answer.at[other, core], answer_sem)
-    merged_out[...] = jnp.transpose(jnp.concatenate([answer[0, core], answer[1, core]], axis=0))
-    merged_copy = pltpu.make_async_copy(merged_out, merged, local_sem.at[1])
-    merged_copy.start()
+    merged[...] = jnp.transpose(jnp.concatenate([answer[0, core], answer[1, core]], axis=0))
 
     await_bytes(partner_part, send_sem.at[0])
     await_bytes(matrix.at[:, 0], send_sem.at[1])
@@ -403,25 +399,21 @@
     await_bytes(sums.at[pl.ds(0, CHIPS - 1)], send_sem.at[8])
     await_bytes(answer.at[0, 0], send_sem.at[9])
     await_bytes(totals.at[pl.ds(0, 2 * groups - 1)], send_sem.at[10])
-    merged_copy.wait()
     await_bytes(totals.at[pl.ds(0, 2 * groups - 1)], totals_sem)
     over_all = jnp.sum(totals[...], axis=0)
-    ratio_out[...] = jnp.sqrt(over_all[:, 0:1] / over_all[:, 1:2]) + jnp.zeros((1, ROWS), F32)
-    ratio_copy = pltpu.make_async_copy(ratio_out, ratio, local_sem.at[0])
-    ratio_copy.start()
-    ratio_copy.wait()
+    ratio[...] = jnp.sqrt(over_all[:, 0:1] / over_all[:, 1:2]) + jnp.zeros((1, ROWS), F32)
 
 
 def local(expert_grams, expert_weights):
     groups = lax.axis_size("grp")
     hbm = pl.BlockSpec(memory_space=pltpu.HBM)
-    anywhere = pl.BlockSpec(memory_space=pl.ANY)
+    vmem = pl.BlockSpec(memory_space=pltpu.VMEM)
     dma = pltpu.SemaphoreType.DMA
     merged, ratio = pl.pallas_call(
         kernel,
         out_shape=(jax.ShapeDtypeStruct((ROWS, COLS), F32), jax.ShapeDtypeStruct((1, ROWS), F32)),
         in_specs=[hbm, hbm],
-        out_specs=(anywhere, anywhere),
+        out_specs=(vmem, vmem),
         scratch_shapes=[
             pltpu.VMEM((CHIPS, EXPERTS, ROWS, WIDE), F32),
             pltpu.VMEM((CHIPS, 2, 2, ROWS, WIDE), BF16),
@@ -443,19 +435,17 @@
             pltpu.VMEM((CHIPS, 4, ROWS), F32),
             pltpu.VMEM((2 * groups, 1, ROWS), F32),
             pltpu.VMEM((2, 2, MINE, ROWS), F32),
-            pltpu.VMEM((ROWS, COLS), F32),
-            pltpu.VMEM((1, ROWS), F32),
-            dma((CHIPS,)),
-            dma((CHIPS,)),
+            dma((CHIPS // GROUP,)),
+            dma((CHIPS // GROUP,)),
             dma,
-            dma((2, SIDE, SIDE)),
             dma((2, SIDE)),
+            dma((2,)),
             dma((4, 10)),
             dma,
             dma,
             dma,
             dma((11,)),
-            dma((2,)),
+            dma((1,)),
             pltpu.SemaphoreType.REGULAR((2,)),
         ],
         compiler_params=pltpu.CompilerParams(

time: 74.4 us -> 73.7 us (level)
  no operation moved by 1% of the time
where the time goes in v5:
time: 73.7 us; the launch traced here: 73.6 us
  Pallas kernels  71.2 us (97%)
  between operations  1.8 us (2%)
    pallas_call x1, Pallas kernels, local(): pl.pallas_call(kernel, out_shape=(jax.ShapeDtypeStruct((ROWS, COLS), F32)...  71.2 us

profile of v5, /device:TPU:1, one launch (start us, length us, event | category | flops | bytes accessed | tf_op | source)
XLA Modules:
  0.0 73.6 jit_solution(16537788788610103908)
XLA Ops:
  0.6 71.2 %merge.1 = (f32[128,128]{1,0:T(8,128)S(1)}, f32[1,128]{1,0:T(1,128)S(1)}) custom-call(f32[4,128,4096]{2,1,0:T(8,128)} %grams.1, bf16[4,128,128]{2,1,0:T(8,128)(2,1)} %weights.1), custom_call_target="tpu_custom_call" | custom-call | tf_op jit(solution)/shard_map/merge/pallas_call | solution.py:412
  71.8 0.6 copy.6

commit v6 on v5

--- a/solution.py
+++ b/solution.py
@@ -27,7 +27,7 @@
     gather_b, gather_0, gather_1, gather_2, residual, mapped_dir, dots, product,
     sums, totals, answer,
     panel_sem, partner_sem, matrix_sem, first_sem, second_sem, gather_sem, sums_sem, totals_sem, answer_sem,
-    send_sem, local_sem, token_sem,
+    send_sem, local_sem, token_sem, turn_sem,
 ):
     grp, row = lax.axis_index("grp"), lax.axis_index("row")
     core, chip = lax.rem(row, 2), lax.div(row, 2)
@@ -207,6 +207,12 @@
                     buffer[chip, half, 1] = low[here]
                 else:
                     buffer[chip, half] = high[here]
+            if self.index > 0:
+
+                @pl.when(core == 1)
+                def _():
+                    pl.semaphore_wait(turn_sem, 1)
+
             for d in (2, 1, 3):
                 self.send(0, 0, 0, d, 0)
                 self.send(0, 0, 1, 0, d)
@@ -225,6 +231,11 @@
                 self.arrive(3 + d, half_block)
                 for e in (2, 1, 3):
                     self.send(0, d, 1, e, 0)
+
+        def pass_turn(self):
+            @pl.when(core == 0)
+            def _():
+                pl.semaphore_signal(turn_sem, 1, device_id=partner, device_id_type=MESH)
 
         def near(self):
             self.arrive(7, self.buffer.at[pl.ds(0, 3)])
@@ -279,6 +290,8 @@
         gather.middle()
         product[:height] = product[:height] + products(gather, planes, middle_blocks, first_time)
         gather.far()
+        if gather.index < 3:
+            gather.pass_turn()
         product[:height] = product[:height] + products(gather, planes, far_blocks, first_time)
         gather.last()
         total = product[:height] + products(gather, planes, [(2, 2)], first_time)
@@ -300,6 +313,7 @@
     for step, (buffer, planes) in enumerate(((gather_0, 2), (gather_1, 2), (gather_2, 1))):
         gather = Gather(step + 1, buffer)
         gather.start(own_w)
+        gather.start_rest()
         if step > 0:
             before, before_planes = ((gather_0, 2), (gather_1, 2))[step - 1]
 
@@ -315,7 +329,6 @@
             following = column_sum(lax.fori_loop(0, CHIPS, advance, zero))
             beta = following / norm
             norm = following
-        gather.start_rest()
         own_u, overlap = finish(gather, planes)
         if step == 0:
             alpha = norm / overlap
@@ -331,6 +344,29 @@
         own_r = own_r - alpha * own_s
         own_w = own_w - alpha * own_t
 
+    alpha_beta = alpha * beta
+    close = own_r - alpha * own_w - alpha_beta * own_s
+    lane = lax.broadcasted_iota(jnp.int32, (MINE, ROWS), 1)
+
+    def pack(columns):
+        packed = jnp.zeros((MINE, ROWS), F32)
+        for i, column in enumerate(columns):
+            packed = jnp.where(lane == i, column, packed)
+        return packed
+
+    def lay_flat(left, right):
+        return jnp.transpose(jnp.concatenate([pack(left), pack(right)], axis=0))
+
+    sums[chip] = lay_flat(
+        [column_sum(t) for t in (own_r * own_w, close * close, close * own_w, close * own_s)],
+        [column_sum(t) for t in (own_w * own_w, own_w * own_s, own_s * own_s)],
+    )[:4]
+
+    def tell_chip(n, _):
+        push(sums.at[chip], sums.at[chip], send_sem.at[8], sums_sem, device(lax.rem(chip + n, CHIPS)))
+        return 0
+
+    lax.fori_loop(1, CHIPS, tell_chip, 0)
     def last_advance(origin, total):
         direction = whole(gather_2, 1, origin) + beta * mapped_dir[origin]
         block = residual[origin] - alpha * direction
@@ -339,34 +375,19 @@
     following = column_sum(lax.fori_loop(0, CHIPS, last_advance, zero))
     beta = following / norm
     norm = following
-
-    own_s = own_w + beta * own_s
     own_p = own_r + beta * own_p
-    close = own_r - alpha * own_s
-    lane = lax.broadcasted_iota(jnp.int32, (MINE, ROWS), 1)
-    def lay_flat(columns):
-        packed = jnp.zeros((MINE, ROWS), F32)
-        for i, column in enumerate(columns):
-            packed = jnp.where(lane == i, column, packed)
-        return jnp.transpose(jnp.concatenate([packed, jnp.zeros_like(packed)], axis=0))[: len(columns)]
-
-    sums[chip] = lay_flat([column_sum(t) for t in (own_r * own_w, close * close, close * own_s, own_s * own_s)])
-
-    def tell_chip(n, _):
-        push(sums.at[chip], sums.at[chip], send_sem.at[8], sums_sem, device(lax.rem(chip + n, CHIPS)))
-        return 0
-
-    lax.fori_loop(1, CHIPS, tell_chip, 0)
     hear_z(1)
-    known = lay_flat([norm, beta, alpha, initial])
+    known = lay_flat([norm, beta, alpha, initial, alpha_beta], [])
     used = lax.broadcasted_iota(jnp.int32, (1, ROWS), 1) < MINE
-    norm, beta, alpha, initial = (jnp.where(used, known[i : i + 1], 1.0) for i in range(4))
+    norm, beta, alpha, initial, alpha_beta = (jnp.where(used, known[i : i + 1], 1.0) for i in range(5))
     await_bytes(sums.at[pl.ds(0, CHIPS - 1)], sums_sem)
-    gathered = jnp.where(used, jnp.sum(sums[...], axis=0), 1.0)
-    overlap, close_close, close_s, s_s = (gathered[i : i + 1] for i in range(4))
+    gathered = jnp.sum(sums[...], axis=0)
+    gathered = jnp.concatenate([gathered, pltpu.roll(gathered, MINE, 1)], axis=0)
+    overlap, c_c, c_w, c_s, w_w, w_s, s_s = (jnp.where(used, gathered[i : i + 1], 1.0) for i in range(7))
     last = norm / jnp.where(used, overlap - beta * norm / alpha, 1.0)
-    excess = last - alpha
-    final = jnp.maximum(close_close - 2.0 * excess * close_s + excess * excess * s_s, 0.0)
+    more_w, more_s = last - alpha, last * beta - alpha_beta
+    final = c_c - 2.0 * (more_w * c_w + more_s * c_s) + more_w * more_w * w_w
+    final = jnp.maximum(final + more_s * (2.0 * more_w * w_s + more_s * s_s), 0.0)
 
     place = grp * 2 + core
     final = column_sum(jnp.where(used, final, 0.0))
@@ -447,6 +468,7 @@
             dma((11,)),
             dma((1,)),
             pltpu.SemaphoreType.REGULAR((2,)),
+            pltpu.SemaphoreType.REGULAR,
         ],
         compiler_params=pltpu.CompilerParams(
             collective_id=0, has_side_effects=True, vmem_limit_bytes=55040 * 1024

time: 73.7 us -> 72.7 us (0.986)
  Pallas kernels: 71.2 us -> 70.2 us
    pallas_call x1, Pallas kernels: 71.2 us -> 70.2 us  [local(): pl.pallas_call(kernel, out_shape=(jax.ShapeDtypeStruct((ROWS, COLS), F32)...]
where the time goes in v6:
time: 72.7 us
  Pallas kernels  70.2 us (97%)
  between operations  1.8 us (2%)
    pallas_call x1, Pallas kernels, local(): pl.pallas_call(kernel, out_shape=(jax.ShapeDtypeStruct((ROWS, COLS), F32)...  70.2 us

profile of v6, /device:TPU:1, one launch (start us, length us, event | category | flops | bytes accessed | tf_op | source)
XLA Modules:
  0.0 72.7 jit_solution(16298132354802283081)
XLA Ops:
  0.6 70.2 %merge.1 = (f32[128,128]{1,0:T(8,128)S(1)}, f32[1,128]{1,0:T(1,128)S(1)}) custom-call(f32[4,128,4096]{2,1,0:T(8,128)} %grams.1, bf16[4,128,128]{2,1,0:T(8,128)(2,1)} %weights.1), custom_call_target="tpu_custom_call" | custom-call | tf_op jit(solution)/shard_map/merge/pallas_call | solution.py:433
  70.9 0.6 copy.6

commit v7 on v6

--- a/solution.py
+++ b/solution.py
@@ -164,15 +164,6 @@
 
     lax.fori_loop(0, CHIPS, send_matrix, 0)
 
-    pieces = []
-    for half in (0, 1):
-        along = y if half == 0 else x
-        total, _ = first_sum(half, 0)
-        await_bytes(second.at[half, 1, pl.ds(0, SIDE - 1)], second_sem.at[half])
-        for j in (1, 3, 2):
-            total = total + second[half, 1, lax.rem(along + j, SIDE)]
-        pieces.append(total)
-    own_r = jnp.concatenate(pieces, axis=0)
 
     near_blocks = [(0, 0), (1, 0), (3, 0), (0, 1), (0, 3), (2, 0), (0, 2)]
     middle_blocks = [(1, 1), (1, 3), (3, 1), (3, 3)]
@@ -196,6 +187,11 @@
 
         def arrive(self, place, ref):
             await_bytes(ref, gather_sem.at[self.index, place])
+
+        def start_half(self, half, value):
+            self.buffer[chip, half, 0], self.buffer[chip, half, 1] = split(value)
+            for d in (2, 1, 3):
+                self.send(0, 0, half, *((d, 0) if half == 0 else (0, d)))
 
         def start(self, value):
             buffer = self.buffer
@@ -300,7 +296,17 @@
     zero = jnp.zeros((MINE, WIDE), F32)
 
     gather = Gather(0, gather_b)
-    gather.start(own_r)
+    pieces = []
+    for half in (0, 1):
+        along = y if half == 0 else x
+        total, _ = first_sum(half, 0)
+        await_bytes(second.at[half, 1, pl.ds(0, SIDE - 1)], second_sem.at[half])
+        for j in (1, 3, 2):
+            total = total + second[half, 1, lax.rem(along + j, SIDE)]
+        pieces.append(total)
+        gather.start_half(half, total)
+    own_r = jnp.concatenate(pieces, axis=0)
+
     hear_z(0)
     tell_z(1)
     await_bytes(matrix.at[:, other], matrix_sem)

time: 72.7 us -> 72.9 us (level)
  no operation moved by 1% of the time
where the time goes in v7:
time: 72.9 us; the launch traced here: 72.8 us
  Pallas kernels  70.4 us (97%)
  between operations  1.8 us (2%)
    pallas_call x1, Pallas kernels, local(): pl.pallas_call(kernel, out_shape=(jax.ShapeDtypeStruct((ROWS, COLS), F32)...  70.4 us

profile of v7, /device:TPU:1, one launch (start us, length us, event | category | flops | bytes accessed | tf_op | source)
XLA Modules:
  0.0 72.8 jit_solution(10094039408512557462)
XLA Ops:
  0.6 70.4 %merge.1 = (f32[128,128]{1,0:T(8,128)S(1)}, f32[1,128]{1,0:T(1,128)S(1)}) custom-call(f32[4,128,4096]{2,1,0:T(8,128)} %grams.1, bf16[4,128,128]{2,1,0:T(8,128)(2,1)} %weights.1), custom_call_target="tpu_custom_call" | custom-call | tf_op jit(solution)/shard_map/merge/pallas_call | solution.py:439
  71.0 0.6 copy.6
